TPU v7x, 32 devices: a whole 2x2x4 slice. The times are simulated.
32 devices in a mesh: row: 8 (over z, core), col: 4 (over y, x).
Axes of the slice: x: 2, y: 2, z: 4, core: 2. Of those that a mesh axis runs over, the one named last changes fastest.
Arguments:
- matrix: bfloat16 [4096, 4096], P('row', 'col'), may hold values from -6 to 6
- factors: float32 [4096, 4096], P('row', 'col')
- inverse: bfloat16 [32, 128, 128], P('col'), may hold values from -0.007171631 to 0.007171631
- pattern: int32 [32, 32], P('row', 'col'), may hold values from 0 to 1, as said below
- dropped: int32 [32, 32], P('row', 'col'), may hold values from 0 to 1, as said below
Outputs:
- factors_out: float32 [4096, 4096], P('row', 'col')
Inputs may be any that keep to these rules, and one draw needn't show every extreme that they name: Block (I, J) can be in the pattern only where I - J is 0, 1, -1, 4, -4, 16 or -16; the blocks with I - J of 0, 1, -1, 4 and -4 are always in it. In each device's region of 4 block rows by 8 block columns, every block column holds at most 3 pattern blocks (exactly 3 in some columns), and every block row at most 2 pattern blocks below the block diagonal (exactly 2 in some rows). `dropped`: dropped blocks lie in the pattern and off the block diagonal.
All inputs are finite; a program needn't handle non-finite values.
Results may differ from a plain program's by a relative error of at most 0.00083.
Values may be sent and summed in bfloat16 or wider, within the bound.
A program may use at most 128 MiB of HBM per device.

v0:
```python
import functools

import jax
import jax.numpy as jnp
from jax import lax
from jax.experimental import pallas as pl
from jax.experimental.pallas import tpu as pltpu
from jax.sharding import PartitionSpec as P

SWEEPS = 2
MESH = pl.DeviceIdType.MESH
F32 = jnp.float32
BF16 = jnp.bfloat16

SLOTS = 4
DIAG, LEFT, RIGHT, OUTER = range(SLOTS)
D_NEAR, D_FAR, L_NEAR, U_NEAR, L_FAR, U_FAR = range(6)


def dot(x, y):
    return jnp.dot(x, y, preferred_element_type=F32)


def sweep_kernel(
    rows, cols, row_devices, col_devices, bs,
    pattern, dropped, matrix, factors, inverse_in, out,
    a, inverse, lb, ub, sd, rd, rln, run, rlf, ruf, acc,
    load_sem, inverse_sem, send_sem, recv_sem,
):
    r, c = lax.axis_index("row"), lax.axis_index("col")
    far_r, far_c = row_devices // 2, col_devices // 2
    q = r - (cols // rows) * c
    barrier = pltpu.get_barrier_semaphore()

    def loads(i, s, j):
        k = i * SLOTS + s
        src = (pl.ds(i * bs, bs), pl.ds(pl.multiple_of(j * bs, bs), bs))
        return (
            pltpu.make_async_copy(factors.at[src], out.at[k], load_sem.at[0, k]),
            pltpu.make_async_copy(matrix.at[src], a.at[k], load_sem.at[1, k]),
        )

    def start_loads(blocks):
        for block in blocks:
            for copy in loads(*block):
                copy.start()

    def wait_loads(blocks):
        for block in blocks:
            for copy in loads(*block):
                copy.wait()

    inverse_copy = pltpu.make_async_copy(inverse_in, inverse, inverse_sem)

    def hello(r2, c2):
        pl.semaphore_signal(barrier, inc=1, device_id=(r2, c2), device_id_type=MESH)

    def message(kind, v, src, dst, slot, r2, c2):
        return pltpu.make_async_remote_copy(
            src_ref=src, dst_ref=dst,
            send_sem=send_sem.at[kind, v], recv_sem=recv_sem.at[slot, v],
            device_id=(r2, c2), device_id_type=MESH,
        )

    def d_near(v):
        return message(D_NEAR, v, sd.at[v], rd.at[v], D_NEAR, r + 1, c)

    def d_far(v):
        return message(D_FAR, v, sd.at[v], rd.at[v], D_NEAR, r + far_r, c)

    def l_near(v):
        return message(L_NEAR, v, lb.at[v, pl.ds(0, rows + 1)], rln.at[v], L_NEAR, r, c + 1)

    def u_near(v):
        return message(U_NEAR, v, ub.at[v, pl.ds(0, rows + 1)], run.at[v], U_NEAR, r + 1, c)

    def l_far(v):
        return message(L_FAR, v, lb.at[v, pl.ds(0, rows)], rlf.at[v], L_FAR, r, c + far_c)

    def u_far(v):
        return message(U_FAR, v, ub.at[v, pl.ds(0, rows)], ruf.at[v], U_FAR, r + far_r, c)

    def lower_step(k, b, v, diag, j, mask=None):
        product = dot(lb[v, b], diag)
        residual = a[k].astype(F32) - product
        if mask is not None:
            residual = residual * mask
        correction = dot(residual.astype(BF16), inverse[j])
        if mask is not None:
            correction = correction * mask
        out[k] = out[k] + correction
        if v + 1 < SWEEPS:
            lb[v + 1, b] = out[k].astype(BF16)

    def upper_steps(k, b, mask=None):
        for v in range(SWEEPS):
            ub[v, b] = out[k].astype(BF16)
            residual = a[k].astype(F32) - out[k]
            if mask is not None:
                residual = residual * mask
            out[k] = out[k] + residual

    def keep(i, s, j):
        k = i * SLOTS + s
        out[k] = out[k] * (1 - dropped[i, j]).astype(F32)

    out[rows * SLOTS] = jnp.zeros((bs, bs), F32)

    def diagonal_owner(h):
        base = h * rows
        below = [(i, LEFT, base + i - 1) for i in range(rows) if base + i >= 1]
        right = [(i, RIGHT, base + i + 1) for i in range(rows) if base + i + 1 < cols]
        diag = [(i, DIAG, base + i) for i in range(rows)]
        outer = [(i, OUTER, i if h else rows + i) for i in range(rows)]
        has_far = c >= far_c
        sends_far = c < far_c
        has_near = c >= 1
        sends_near = c + 1 < col_devices

        def when_near_in(f):
            if h:
                f()
            else:
                pl.when(has_near)(f)

        def when_near_out(f):
            if h:
                pl.when(sends_near)(f)
            else:
                f()

        start_loads(diag)
        start_loads(outer)
        start_loads(right)
        start_loads(below)
        inverse_copy.start()

        def hello_near():
            hello(r - 1, c)
            if not h:
                hello(r, c - 1)

        when_near_in(hello_near)

        @pl.when(has_far)
        def _():
            hello(r - far_r, c)
            hello(r, c - far_c)

        wait_loads(diag)
        for i in range(rows):
            sd[0, i] = out[i * SLOTS + DIAG].astype(BF16)
        near_peers = sends_near.astype(jnp.int32) if h else 1
        peers = near_peers + sends_far.astype(jnp.int32)
        pl.when(peers > 0)(lambda: pl.semaphore_wait(barrier, peers))

        def send_d(v):
            pl.when(sends_far)(lambda: d_far(v).start())
            when_near_out(lambda: d_near(v).start())

        send_d(0)
        wait_loads(outer)
        wait_loads(right)
        for i, s, j in right:
            upper_steps(i * SLOTS + s, 2 * rows - 1 - i)
        if not h:
            for i, s, j in outer:
                upper_steps(i * SLOTS + s, i)
            u_near(0).start()
            u_near(1).start()
        wait_loads(below)
        for i, s, j in below:
            lb[0, rows + i] = out[i * SLOTS + s].astype(BF16)
        if h:
            for i, s, j in outer:
                lb[0, i] = out[i * SLOTS + s].astype(BF16)
        inverse_copy.wait()

        for v in range(SWEEPS):
            acc[0] = jnp.zeros((bs, bs), F32)
            for i in range(1, rows):
                acc[i] = dot(lb[v, rows + i], ub[v, 2 * rows - i])

            def near_terms():
                u_near_in = message(U_NEAR, v, ub.at[v, pl.ds(0, rows + 1)], run.at[v], U_NEAR, r - 1, c)
                u_near_in.wait_recv()
                if h:
                    left = lb
                else:
                    message(L_NEAR, v, lb.at[v, pl.ds(0, rows + 1)], rln.at[v], L_NEAR, r, c - 1).wait_recv()
                    left = rln
                acc[0] = acc[0] + dot(left[v, rows], run[v, rows])
                for i in range(rows):
                    acc[i] = acc[i] + dot(left[v, i], run[v, i])

            def far_terms():
                message(U_FAR, v, ub.at[v, pl.ds(0, rows)], ruf.at[v], U_FAR, r - far_r, c).wait_recv()
                message(L_FAR, v, lb.at[v, pl.ds(0, rows)], rlf.at[v], L_FAR, r, c - far_c).wait_recv()
                for i in range(rows):
                    acc[i] = acc[i] + dot(rlf[v, i], ruf[v, i])

            def local_lower():
                for i in range(1, rows):
                    lower_step(i * SLOTS + LEFT, rows + i, v, sd[v, i - 1], base + i - 1)

            def lower_from_before():
                if h:
                    message(D_NEAR, v, sd.at[v], rd.at[v], D_NEAR, r - 1, c).wait_recv()
                    lower_step(LEFT, rows, v, rd[v, rows - 1], rows - 1)
                    for i in range(rows):
                        lower_step(i * SLOTS + OUTER, i, v, rd[v, i], i)

            def diag_step():
                for i in range(rows):
                    k = i * SLOTS + DIAG
                    residual = a[k].astype(F32) - acc[i] - out[k]
                    out[k] = out[k] + residual
                    if v + 1 < SWEEPS:
                        sd[v + 1, i] = out[k].astype(BF16)
                if v + 1 < SWEEPS:
                    send_d(v + 1)

            local_lower()
            when_near_in(near_terms)
            if v + 1 < SWEEPS:
                pl.when(has_far)(far_terms)
                diag_step()
                lower_from_before()
            else:
                lower_from_before()
                pl.when(has_far)(far_terms)
                diag_step()

        for i, s, j in below + right + outer:
            keep(i, s, j)
        for v in range(SWEEPS):
            when_near_out(lambda: d_near(v).wait_send())
            pl.when(sends_far)(lambda: d_far(v).wait_send())
            if not h:
                u_near(v).wait_send()

    def lower_owner(blocks, source_r, l_message, far):
        places = [(i, s, j) for i, s, j, b, n in blocks]
        start_loads(places)
        inverse_copy.start()
        hello(source_r, c)
        wait_loads(places)
        masks = {}
        for i, s, j, b, n in blocks:
            k = i * SLOTS + s
            masks[k] = pattern[i, j].astype(F32) if far else None
            if far:
                out[k] = out[k] * masks[k]
            lb[0, b] = out[k].astype(BF16)
        pl.semaphore_wait(barrier, 1)
        l_message(0).start()
        inverse_copy.wait()
        for v in range(SWEEPS):
            message(D_NEAR, v, sd.at[v], rd.at[v], D_NEAR, source_r, c).wait_recv()
            for i, s, j, b, n in blocks:
                k = i * SLOTS + s
                lower_step(k, b, v, rd[v, n], j, masks[k])
            if v + 1 < SWEEPS:
                l_message(v + 1).start()
        for i, s, j in places:
            keep(i, s, j)
        for v in range(SWEEPS):
            l_message(v).wait_send()

    def upper_owner(blocks, u_message, far):
        places = [(i, s, j) for i, s, j, b in blocks]
        start_loads(places)
        wait_loads(places)
        for i, s, j, b in blocks:
            k = i * SLOTS + s
            mask = pattern[i, j].astype(F32) if far else None
            if far:
                out[k] = out[k] * mask
            upper_steps(k, b, mask)
        pl.semaphore_wait(barrier, 1)
        for v in range(SWEEPS):
            u_message(v).start()
        for i, s, j in places:
            keep(i, s, j)
        for v in range(SWEEPS):
            u_message(v).wait_send()

    pl.when(q == 0)(lambda: diagonal_owner(0))
    pl.when(q == 1)(lambda: diagonal_owner(1))

    @pl.when(q == 2)
    def _():
        blocks = [(i, OUTER, rows + i, i, i) for i in range(rows)]
        lower_owner(blocks + [(0, LEFT, cols - 1, rows, rows - 1)], r - 1, l_near, False)

    @pl.when(q == -1)
    def _():
        blocks = [(i, OUTER, i, i) for i in range(rows)]
        upper_owner(blocks + [(rows - 1, RIGHT, 0, rows)], u_near, False)

    @pl.when((q == far_r) | (q == far_r + 1))
    def _():
        base = (q - far_r) * rows
        blocks = [(i, OUTER, base + i, i, i) for i in range(rows)]
        lower_owner(blocks, r - far_r, l_far, True)

    @pl.when((q == -far_r) | (q == 1 - far_r))
    def _():
        base = (q + far_r) * rows
        blocks = [(i, OUTER, base + i, i) for i in range(rows)]
        upper_owner(blocks, u_far, True)


def place_kernel(rows, cols, row_devices, bs, blocks, out, sem):
    r, c = lax.axis_index("row"), lax.axis_index("col")
    q = r - (cols // rows) * c
    far = (row_devices // 2) * rows
    copies = []
    for i in range(rows):
        for j in range(cols):
            d = rows * q + i - j
            k = jnp.where(
                d == 0, i * SLOTS + DIAG,
                jnp.where(
                    d == 1, i * SLOTS + LEFT,
                    jnp.where(
                        d == -1, i * SLOTS + RIGHT,
                        jnp.where(
                            (d == rows) | (d == -rows) | (d == far) | (d == -far),
                            i * SLOTS + OUTER, rows * SLOTS,
                        ),
                    ),
                ),
            )
            dst = out.at[pl.ds(i * bs, bs), pl.ds(j * bs, bs)]
            copies.append(pltpu.make_async_copy(blocks.at[k], dst, sem.at[i * cols + j]))
    for copy in copies:
        copy.start()
    for copy in copies:
        copy.wait()


def solution(mesh):
    row_devices, col_devices = mesh.shape["row"], mesh.shape["col"]

    def on_device(matrix, factors, inverse, pattern, dropped):
        rows, cols = pattern.shape
        bs = inverse.shape[1]
        places = rows * SLOTS
        half = lambda *n: pltpu.VMEM(n + (bs, bs), BF16)
        hbm = pl.BlockSpec(memory_space=pl.ANY)
        smem = pl.BlockSpec(memory_space=pltpu.SMEM)
        vmem = pl.BlockSpec(memory_space=pltpu.VMEM)
        blocks = pl.pallas_call(
            functools.partial(sweep_kernel, rows, cols, row_devices, col_devices, bs),
            out_shape=jax.ShapeDtypeStruct((places + 1, bs, bs), F32),
            in_specs=[smem, smem, hbm, hbm, hbm],
            out_specs=vmem,
            scratch_shapes=[
                half(places), half(cols), half(SWEEPS, 2 * rows), half(SWEEPS, 2 * rows),
                half(SWEEPS, rows), half(SWEEPS, rows),
                half(SWEEPS, rows + 1), half(SWEEPS, rows + 1), half(SWEEPS, rows), half(SWEEPS, rows),
                pltpu.VMEM((rows, bs, bs), F32),
                pltpu.SemaphoreType.DMA((2, places)),
                pltpu.SemaphoreType.DMA,
                pltpu.SemaphoreType.DMA((6, SWEEPS)),
                pltpu.SemaphoreType.DMA((6, SWEEPS)),
            ],
            compiler_params=pltpu.CompilerParams(collective_id=0, has_side_effects=True),
            name="sweeps",
        )(pattern, dropped, matrix, factors, inverse)
        return pl.pallas_call(
            functools.partial(place_kernel, rows, cols, row_devices, bs),
            out_shape=jax.ShapeDtypeStruct(factors.shape, F32),
            in_specs=[vmem],
            out_specs=hbm,
            scratch_shapes=[pltpu.SemaphoreType.DMA((rows * cols,))],
            name="place",
        )(blocks)

    placed = (P("row", "col"), P("row", "col"), P("col", None, None), P("row", "col"), P("row", "col"))
    return jax.shard_map(
        on_device, mesh=mesh, in_specs=placed, out_specs=P("row", "col"), check_vma=False
    )
```

profile of v0, /device:TPU:20, one launch (start us, length us, event | category | flops | bytes accessed | tf_op | source)
XLA Modules:
  0.0 18.4 jit_solution(7815382553992503352)
XLA Ops:
  0.0 15.6 %sweeps.1.blocks = f32[17,128,128]{2,1,0:T(8,128)} custom-call(s32[4,8]{1,0:T(4,128)} %pattern.1, s32[4,8]{1,0:T(4,128)} %dropped.1, bf16[512,1024]{1,0:T(8,128)(2,1)} %matrix.1, f32[512,1024]{1,0:T(8,128)} %factors.1, bf16[8,128,128]{2,1,0:T(8,128)(2,1)} %inverse_in.1), custom_call_target="tpu_custom_call" | custom-call | tf_op jit(solution)/shard_map/sweeps/pallas_call | solution.py:354
  15.6 2.8 %place.1 = f32[512,1024]{1,0:T(8,128)} custom-call(f32[17,128,128]{2,1,0:T(8,128)} %sweeps.1.blocks), custom_call_target="tpu_custom_call" | custom-call | tf_op jit(solution)/shard_map/place/pallas_call | solution.py:372
where the time goes:
time: 18.6 us; the launch traced here: 18.4 us
  Pallas kernels  18.4 us (99%)
    pallas_call x1, Pallas kernels, on_device(): pl.pallas_call(functools.partial(sweep_kernel, rows, cols, row_devices, c...  15.6 us
    pallas_call x1, Pallas kernels, on_device(): pl.pallas_call(functools.partial(place_kernel, rows, cols, row_devices, b...  2.81 us

commit v1 on v0

--- a/solution.py
+++ b/solution.py
@@ -23,8 +23,8 @@
 
 def sweep_kernel(
     rows, cols, row_devices, col_devices, bs,
-    pattern, dropped, matrix, factors, inverse_in, out,
-    a, inverse, lb, ub, sd, rd, rln, run, rlf, ruf, acc,
+    pattern_in, dropped_in, matrix, factors, inverse_in, out,
+    pattern, dropped, flag_sem, a, inverse, lb, ub, sd, rd, rln, run, rlf, ruf, acc,
     load_sem, inverse_sem, send_sem, recv_sem,
 ):
     r, c = lax.axis_index("row"), lax.axis_index("col")
@@ -50,6 +50,12 @@
             for copy in loads(*block):
                 copy.wait()
 
+    flag_copies = (
+        pltpu.make_async_copy(pattern_in, pattern, flag_sem.at[0]),
+        pltpu.make_async_copy(dropped_in, dropped, flag_sem.at[1]),
+    )
+    for copy in flag_copies:
+        copy.start()
     inverse_copy = pltpu.make_async_copy(inverse_in, inverse, inverse_sem)
 
     def hello(r2, c2):
@@ -99,6 +105,9 @@
             if mask is not None:
                 residual = residual * mask
             out[k] = out[k] + residual
+
+    def wait_flag(n):
+        flag_copies[n].wait()
 
     def keep(i, s, j):
         k = i * SLOTS + s
@@ -231,6 +240,8 @@
                 pl.when(has_far)(far_terms)
                 diag_step()
 
+        wait_flag(0)
+        wait_flag(1)
         for i, s, j in below + right + outer:
             keep(i, s, j)
         for v in range(SWEEPS):
@@ -245,6 +256,7 @@
         inverse_copy.start()
         hello(source_r, c)
         wait_loads(places)
+        wait_flag(0)
         masks = {}
         for i, s, j, b, n in blocks:
             k = i * SLOTS + s
@@ -262,6 +274,7 @@
                 lower_step(k, b, v, rd[v, n], j, masks[k])
             if v + 1 < SWEEPS:
                 l_message(v + 1).start()
+        wait_flag(1)
         for i, s, j in places:
             keep(i, s, j)
         for v in range(SWEEPS):
@@ -271,6 +284,7 @@
         places = [(i, s, j) for i, s, j, b in blocks]
         start_loads(places)
         wait_loads(places)
+        wait_flag(0)
         for i, s, j, b in blocks:
             k = i * SLOTS + s
             mask = pattern[i, j].astype(F32) if far else None
@@ -280,10 +294,21 @@
         pl.semaphore_wait(barrier, 1)
         for v in range(SWEEPS):
             u_message(v).start()
+        wait_flag(1)
         for i, s, j in places:
             keep(i, s, j)
         for v in range(SWEEPS):
             u_message(v).wait_send()
+
+    far_roles = [q == k for f in (-far_r, far_r) for k in (f, f + 1)]
+    idle = ~((q >= -1) & (q <= 2))
+    for role in far_roles:
+        idle = idle & ~role
+
+    @pl.when(idle)
+    def _():
+        wait_flag(0)
+        wait_flag(1)
 
     pl.when(q == 0)(lambda: diagonal_owner(0))
     pl.when(q == 1)(lambda: diagonal_owner(1))
@@ -349,14 +374,15 @@
         places = rows * SLOTS
         half = lambda *n: pltpu.VMEM(n + (bs, bs), BF16)
         hbm = pl.BlockSpec(memory_space=pl.ANY)
-        smem = pl.BlockSpec(memory_space=pltpu.SMEM)
         vmem = pl.BlockSpec(memory_space=pltpu.VMEM)
         blocks = pl.pallas_call(
             functools.partial(sweep_kernel, rows, cols, row_devices, col_devices, bs),
-            out_shape=jax.ShapeDtypeStruct((places + 1, bs, bs), F32),
-            in_specs=[smem, smem, hbm, hbm, hbm],
+            out_shape=pltpu.VMEM((places + 1, bs, bs), F32),
+            in_specs=[hbm] * 5,
             out_specs=vmem,
             scratch_shapes=[
+                pltpu.SMEM((rows, cols), jnp.int32), pltpu.SMEM((rows, cols), jnp.int32),
+                pltpu.SemaphoreType.DMA((2,)),
                 half(places), half(cols), half(SWEEPS, 2 * rows), half(SWEEPS, 2 * rows),
                 half(SWEEPS, rows), half(SWEEPS, rows),
                 half(SWEEPS, rows + 1), half(SWEEPS, rows + 1), half(SWEEPS, rows), half(SWEEPS, rows),
@@ -376,7 +402,7 @@
             out_specs=hbm,
             scratch_shapes=[pltpu.SemaphoreType.DMA((rows * cols,))],
             name="place",
-        )(blocks)
+        )(pltpu.with_memory_space_constraint(blocks, pltpu.VMEM))
 
     placed = (P("row", "col"), P("row", "col"), P("col", None, None), P("row", "col"), P("row", "col"))
     return jax.shard_map(

time: 18.6 us -> 15.7 us (0.84)
  Pallas kernels: 18.4 us -> 15.5 us
    pallas_call x1, Pallas kernels: 15.6 us -> 13.9 us  [on_device(): pl.pallas_call(functools.partial(sweep_kernel, rows, cols, row_devices, c...]
    pallas_call x1, Pallas kernels: 2.81 us -> 1.59 us  [on_device(): pl.pallas_call(functools.partial(place_kernel, rows, cols, row_devices, b...]
where the time goes in v1:
time: 15.7 us; the launch traced here: 15.5 us
  Pallas kernels  15.5 us (99%)
    pallas_call x1, Pallas kernels, on_device(): pl.pallas_call(functools.partial(sweep_kernel, rows, cols, row_devices, c...  13.9 us
    pallas_call x1, Pallas kernels, on_device(): pl.pallas_call(functools.partial(place_kernel, rows, cols, row_devices, b...  1.59 us

profile of v1, /device:TPU:20, one launch (start us, length us, event | category | flops | bytes accessed | tf_op | source)
XLA Modules:
  0.0 15.5 jit_solution(7198638995015662913)
XLA Ops:
  0.0 13.9 %sweeps.1.blocks = f32[17,128,128]{2,1,0:T(8,128)S(1)} custom-call(s32[4,8]{1,0:T(4,128)} %pattern_in.1, s32[4,8]{1,0:T(4,128)} %dropped_in.1, bf16[512,1024]{1,0:T(8,128)(2,1)} %matrix.1, f32[512,1024]{1,0:T(8,128)} %factors.1, bf16[8,128,128]{2,1,0:T(8,128)(2,1)} %inverse_in.1), custom_call_target="tpu_custom_call" | custom-call | tf_op jit(solution)/shard_map/sweeps/pallas_call | solution.py:378
  13.9 1.6 %place.1 = f32[512,1024]{1,0:T(8,128)} custom-call(f32[17,128,128]{2,1,0:T(8,128)S(1)} %sweeps.1.blocks), custom_call_target="tpu_custom_call" | custom-call | tf_op jit(solution)/shard_map/place/pallas_call | solution.py:398

commit v2 on v0

v2 whole, which is shorter than its diff:
```python
import functools

import jax
import jax.numpy as jnp
from jax import lax
from jax.experimental import pallas as pl
from jax.experimental.pallas import tpu as pltpu
from jax.sharding import PartitionSpec as P

SWEEPS = 2
MESH = pl.DeviceIdType.MESH
F32 = jnp.float32
BF16 = jnp.bfloat16

SLOTS = 4
DIAG, LEFT, RIGHT, OUTER = range(SLOTS)
D, L_NEAR, U_NEAR, L_FAR, U_FAR = range(5)

def dot(x, y):
    return jnp.dot(x, y, preferred_element_type=F32)


def sweep_kernel(
    rows, cols, row_devices, col_devices, bs,
    pattern_in, dropped_in, matrix, factors, inverse_in, out,
    pattern, dropped, a, inverse, lb, ub, sd, rd, rln, run, rlf, ruf, acc,
    flag_sem, load_sem, lead_sem, send_sem, recv_sem,
):
    r, c = lax.axis_index("row"), lax.axis_index("col")
    far_r, far_c = row_devices // 2, col_devices // 2
    last = col_devices - 1
    q = r - (cols // rows) * c
    barrier = pltpu.get_barrier_semaphore()
    inbox = {D: rd, L_NEAR: rln, U_NEAR: run, L_FAR: rlf, U_FAR: ruf}
    half = rows // 2

    near = [(0, 1 + half), (1 + half, rows - half)]
    far = [(0, half), (half, rows - half)]
    parts = {
        D: [(n, 1) for n in range(rows)], L_NEAR: [(n, 1) for n in range(rows + 1)],
        U_NEAR: near, L_FAR: far, U_FAR: far,
    }
    first_sem = {D: 0, L_NEAR: 0}
    for kind, before, size in ((U_NEAR, L_NEAR, rows + 1), (L_FAR, U_NEAR, 2), (U_FAR, L_FAR, 2)):
        first_sem[kind] = first_sem[before] + SWEEPS * size

    def arrival(kind, v, p):
        size = rows + 1 if kind in (D, L_NEAR) else 2
        return recv_sem.at[first_sem[kind] + v * size + p]

    def part_of(kind, n):
        return max(p for p, (start, size) in enumerate(parts[kind]) if start <= n)

    pending, seen = [], set()

    def remote(kind, v, p, buf, r2, c2):
        at = (v, pl.ds(*parts[kind][p]))
        return pltpu.make_async_remote_copy(
            src_ref=buf.at[at], dst_ref=inbox[kind].at[at],
            send_sem=send_sem, recv_sem=arrival(kind, v, p),
            device_id=(r2, c2), device_id_type=MESH,
        )

    def send(kind, v, p, buf, r2, c2):
        remote(kind, v, p, buf, r2, c2).start()
        pending.append((kind, v, p, buf))

    def await_part(kind, v, p):
        if (kind, v, p) not in seen:
            seen.add((kind, v, p))
            remote(kind, v, p, inbox[kind], r ^ 1, c).wait_recv()

    def got(kind, v, n):
        await_part(kind, v, part_of(kind, n))
        return inbox[kind][v, n]

    def drain():
        for sent in pending:
            remote(*sent, r ^ 1, c).wait_send()
        pending.clear()
        seen.clear()

    def hello(r2, c2):
        pl.semaphore_signal(barrier, inc=1, device_id=(r2, c2), device_id_type=MESH)

    flag_copies = (
        pltpu.make_async_copy(pattern_in, pattern, flag_sem.at[0]),
        pltpu.make_async_copy(dropped_in, dropped, flag_sem.at[1]),
    )

    def start_flags():
        for copy in flag_copies:
            copy.start()

    FIRST, SECOND, MATRIX, INVERSE = range(4)
    inverse_copy = pltpu.make_async_copy(inverse_in, inverse, load_sem.at[INVERSE])

    def start_loads(group, places):
        source, dest = (matrix, a) if group == MATRIX else (factors, out)
        for i, s, j in places:
            src = (pl.ds(i * bs, bs), pl.ds(pl.multiple_of(j * bs, bs), bs))
            pltpu.make_async_copy(source.at[src], dest.at[i * SLOTS + s], load_sem.at[group]).start()

    def wait_loads(group, places):
        dest = (a if group == MATRIX else out).at[pl.ds(0, len(places))]
        pltpu.make_async_copy(dest, dest, load_sem.at[group]).wait()

    odd = lax.rem(c, 2) == 1

    def lower_step(k, b, v, diag, j, mask=None):
        product = dot(lb[v, b], diag)
        residual = a[k].astype(F32) - product
        if mask is not None:
            residual = residual * mask
        correction = dot(residual.astype(BF16), inverse[j])
        if mask is not None:
            correction = correction * mask
        new = out[k] + correction
        out[k] = new
        if v + 1 < SWEEPS:
            lb[v + 1, b] = new.astype(BF16)

    def upper_steps(k, b, mask=None):
        target, value = a[k].astype(F32), out[k]
        for v in range(SWEEPS):
            residual = target - value
            if mask is not None:
                residual = residual * mask
            value = value + residual
            if v + 1 < SWEEPS:
                ub[v + 1, b] = value.astype(BF16)
        out[k] = value

    def keep(places):
        for i, s, j in places:
            k = i * SLOTS + s
            out[k] = out[k] * (1 - dropped[i, j]).astype(F32)

    def diagonal_owner(h, near_in, far_in, near_out, far_out, detour=False):
        if near_in:
            hello(r - 1, c)
            if not h:
                hello(r, c - 1)
                pl.when(~odd & (c >= 2) & (c < last))(lambda: hello(r + 1, c + 1))
                if far_in:
                    hello(r - 1, c - 2)
        if far_in:
            hello(r - far_r, c)
            hello(r, c - far_c)

        base = h * rows
        left = [(i, LEFT, base + i - 1) for i in range(rows) if base + i >= 1]
        right = [(i, RIGHT, base + i + 1) for i in range(rows) if base + i + 1 < cols]
        diag = [(i, DIAG, base + i) for i in range(rows)]
        outer = [(i, OUTER, i if h else rows + i) for i in range(rows)]
        at_right = lambda i: 0 if i == rows - 1 else 1 + rows + i
        at_left = lambda i: rows + i if i else 0

        start_loads(FIRST, diag)
        start_loads(SECOND, right + outer + left)
        start_loads(MATRIX, right + outer + diag + left)
        inverse_copy.start()
        start_flags()

        wait_loads(FIRST, diag)
        for i in range(rows):
            sd[0, i] = out[i * SLOTS + DIAG].astype(BF16)
        if near_out or far_out:
            pl.semaphore_wait(barrier, near_out + far_out)

        def send_near(v, i):
            if near_out:
                send(D, v, i, sd, r + 1 - detour, c + detour)

        def send_far(v):
            if far_out:
                for i in range(rows):
                    send(D, v, i, sd, r + far_r, c)

        for i in range(rows):
            send_near(0, i)
        send_far(0)

        wait_loads(SECOND, right + outer + left)
        for i, s, j in right:
            ub[0, at_right(i)] = out[i * SLOTS + s].astype(BF16)
        for i, s, j in outer:
            (lb if h else ub)[0, 1 + i] = out[i * SLOTS + s].astype(BF16)
        if not h:
            for p in range(2):
                send(U_NEAR, 0, p, ub, r + 1, c)
        for i, s, j in left:
            lb[0, at_left(i)] = out[i * SLOTS + s].astype(BF16)
        wait_loads(MATRIX, right + outer + diag + left)
        for i, s, j in right if h else right + outer:
            upper_steps(i * SLOTS + s, 1 + i if s == OUTER else at_right(i))
        if not h:
            for p in range(2):
                send(U_NEAR, 1, p, ub, r + 1, c)
        inverse_copy.wait()

        def local_lower(v):
            for i in range(1, rows):
                lower_step(i * SLOTS + LEFT, at_left(i), v, sd[v, i - 1], base + i - 1)

        def lower_from_before(v):
            for i in range(rows):
                from_before = got(D, v, i)
                lower_step(i * SLOTS + OUTER, 1 + i, v, from_before, i)
            lower_step(LEFT, 0, v, from_before, rows - 1)

        def products(v):
            for i in range(1, rows):
                acc[i] = dot(lb[v, at_left(i)], ub[v, at_right(i - 1)])

        def diag_step(v, i):
            k = i * SLOTS + DIAG
            terms = [acc[i]] if i else []
            if near_in:
                for n in (1 + i,) if i else (0, 1):
                    u = got(U_NEAR, v, n)
                    l = lb[v, n] if h else got(L_NEAR, v, n)
                    terms.append(dot(l, u))
            if far_in:
                l = got(L_FAR, v, i)
                u = got(U_FAR, v, i)
                terms.append(dot(l, u))
            old = out[k]
            new = old + (a[k].astype(F32) - sum(terms[1:], terms[0] if terms else jnp.zeros((bs, bs), F32)) - old)
            out[k] = new
            if v + 1 < SWEEPS:
                sd[v + 1, i] = new.astype(BF16)
                send_near(v + 1, i)

        def sweep(v):
            local_lower(v)
            if h:
                lower_from_before(v)
            for i in range(rows) if v + 1 < SWEEPS else (1, 0, *range(2, rows)):
                diag_step(v, i)
            if v + 1 < SWEEPS:
                send_far(v + 1)

        for v in range(SWEEPS):
            pl.when(c >= 0)(lambda: products(v))
            pl.when(c >= 0)(lambda: sweep(v))

        for copy in flag_copies:
            copy.wait()
        keep(left + right + outer)
        drain()

    def lower_owner(blocks, kind, source, target):
        hello(source[0], source[1] + (c == 0).astype(jnp.int32) if kind == L_NEAR else source[1])
        start_flags()
        places = [(i, s, j) for i, s, j, b, n in blocks]
        start_loads(FIRST, places)
        start_loads(MATRIX, places)
        inverse_copy.start()
        if kind == L_FAR:
            flag_copies[0].wait()
        wait_loads(FIRST, places)
        masks = {}
        for i, s, j, b, n in blocks:
            k = i * SLOTS + s
            masks[k] = pattern[i, j].astype(F32) if kind == L_FAR else None
            value = out[k]
            if kind == L_FAR:
                value = value * masks[k]
                out[k] = value
            lb[0, b] = value.astype(BF16)
        detour = (odd & (c + 2 <= last)).astype(jnp.int32) if kind == L_NEAR else 0
        pl.semaphore_wait(barrier, 1 + detour)
        for p in range(len(parts[kind])):
            send(kind, 0, p, lb, *target)
        wait_loads(MATRIX, places)
        inverse_copy.wait()
        for v in range(SWEEPS):
            ds, done = {}, set()
            for i, s, j, b, n in blocks:
                k = i * SLOTS + s
                if n not in ds:
                    ds[n] = got(D, v, n)
                lower_step(k, b, v, ds[n], j, masks[k])
                done.add(b)
                start, size = parts[kind][part_of(kind, b)]
                if v + 1 < SWEEPS and done >= set(range(start, start + size)):
                    send(kind, v + 1, part_of(kind, b), lb, target[0] + detour, target[1] + detour)
        if kind != L_FAR:
            flag_copies[0].wait()
        flag_copies[1].wait()
        keep(places)
        drain()

    def pass_on(kind, v, order, target):
        for p in order:
            await_part(kind, v, p)
            send(kind, v, p, inbox[kind], *target)

    def lead_copies(to, which):
        short = bs // 8
        pieces = ((0, 0, pl.ds(0, short)), (0, 0, pl.ds(short, bs - short)), (0, pl.ds(1, half)))
        return [
            pltpu.make_async_remote_copy(
                src_ref=ub.at[at], dst_ref=run.at[at],
                send_sem=send_sem if n else lead_sem, recv_sem=arrival(U_NEAR, 0, 0),
                device_id=to, device_id_type=MESH,
            )
            for n, at in enumerate(pieces) if n in which
        ]

    def upper_owner(blocks, kind, target, second=None, passes=None):
        if passes is not None:
            when, greeted, body = passes
            pl.when(when)(lambda: hello(*greeted))
        start_flags()
        places = [(i, s, j) for i, s, j, b in blocks]
        start_loads(FIRST, places)
        start_loads(MATRIX, places)
        flag_copies[0].wait()
        wait_loads(FIRST, places)
        masks = {}
        for i, s, j, b in blocks:
            k = i * SLOTS + s
            masks[k] = pattern[i, j].astype(F32) if kind == U_FAR else None
            value = out[k]
            if kind == U_FAR:
                value = value * masks[k]
                out[k] = value
            ub[0, b] = value.astype(BF16)
        peers = 1 + (second is not None or kind == U_FAR)
        if passes is not None:
            peers = peers + when.astype(jnp.int32)
        pl.semaphore_wait(barrier, peers)
        if second is None:
            for p in range(2):
                send(kind, 0, p, ub, *target)
        else:
            for copy in lead_copies(target, (0, 1, 2)):
                copy.start()
            send(kind, 0, 1, ub, *target)
            lead_copies(target, (0,))[0].wait_send()
            for h in (0, 1):
                hello(r + 1 + h - far_r, c)
        wait_loads(MATRIX, places)
        for i, s, j, b in blocks:
            upper_steps(i * SLOTS + s, b, masks[i * SLOTS + s])
        send(kind, 1, 0, ub, *target)
        send(kind, 1, 1, ub, *(second or target))
        flag_copies[1].wait()
        keep(places)
        if passes is not None:
            @pl.when(when)
            def _():
                own = list(pending)
                pending.clear()
                body()
                drain()
                pending.extend(own)
        if second is not None:
            for copy in lead_copies(target, (1, 2)):
                copy.wait_send()
        drain()

    def pass_diagonal():
        for v in range(SWEEPS):
            pass_on(D, v, range(rows), (r + 1, c - 1))

    def near_passer():
        hello(r, c + 2)
        pl.semaphore_wait(barrier, 1)
        pass_on(U_NEAR, 1, (1,), (r + 1, c + 2))
        drain()

    for h in (0, 1):
        pl.when((q == h) & (c == 0))(lambda: diagonal_owner(h, bool(h), False, True, True, bool(h)))
        pl.when((q == h) & (c > 0) & (c < far_c))(lambda: diagonal_owner(h, True, False, True, True))
        pl.when((q == h) & (c >= far_c) & (c < last))(lambda: diagonal_owner(h, True, True, True, False))
        pl.when((q == h) & (c == last))(lambda: diagonal_owner(h, True, True, not h, False))

    near_lower = [(i, OUTER, rows + i, 1 + i, i) for i in range(rows)] + [(0, LEFT, cols - 1, 0, rows - 1)]
    pl.when(q == 2)(lambda: lower_owner(near_lower, L_NEAR, (r - 1, c), (r, c + 1)))

    near_upper = [(rows - 1, RIGHT, 0, 0)] + [(i, OUTER, i, 1 + i) for i in range(rows)]
    pass_lower = (odd & (c >= 3), (r - 1, c - 2), lambda: pass_on(L_NEAR, 1, (*range(1, rows + 1), 0), (r - 1, c - 1)))
    pass_diag = (c == 1, (r, c - 1), pass_diagonal)
    pl.when((q == -1) & (c == 1))(lambda: upper_owner(near_upper, U_NEAR, (r + 1, c), passes=pass_diag))
    pl.when((q == -1) & (c > 1) & (c < far_c))(lambda: upper_owner(near_upper, U_NEAR, (r + 1, c), passes=pass_lower))
    pl.when((q == -1) & (c >= far_c))(
        lambda: upper_owner(near_upper, U_NEAR, (r + 1, c), second=(r, c - 2), passes=pass_lower)
    )
    pl.when((q == 3) & (c + 2 >= far_c) & (c + 2 <= last))(near_passer)
    for h in (0, 1):
        far_lower = [(i, OUTER, h * rows + i, i, i) for i in range(rows)]
        far_upper = [(i, OUTER, h * rows + i, i) for i in range(rows)]
        pl.when(q == far_r + h)(lambda: lower_owner(far_lower, L_FAR, (r - far_r, c), (r, c + far_c)))
        pl.when(q == h - far_r)(
            lambda: upper_owner(far_upper, U_FAR, (r + far_r, c))
        )

    out[rows * SLOTS] = jnp.zeros((bs, bs), F32)


def place_kernel(rows, cols, row_devices, bs, blocks, out, sem):
    r, c = lax.axis_index("row"), lax.axis_index("col")
    q = r - (cols // rows) * c
    far = (row_devices // 2) * rows
    copies = []
    for i in range(rows):
        for j in range(cols):
            d = rows * q + i - j
            k = jnp.where(
                d == 0, i * SLOTS + DIAG,
                jnp.where(
                    d == 1, i * SLOTS + LEFT,
                    jnp.where(
                        d == -1, i * SLOTS + RIGHT,
                        jnp.where(
                            (d == rows) | (d == -rows) | (d == far) | (d == -far),
                            i * SLOTS + OUTER, rows * SLOTS,
                        ),
                    ),
                ),
            )
            dst = out.at[pl.ds(i * bs, bs), pl.ds(j * bs, bs)]
            copies.append(pltpu.make_async_copy(blocks.at[k], dst, sem))
    for copy in copies:
        copy.start()
    pltpu.make_async_copy(out, out, sem).wait()


def solution(mesh):
    row_devices, col_devices = mesh.shape["row"], mesh.shape["col"]

    def on_device(matrix, factors, inverse, pattern, dropped):
        rows, cols = pattern.shape
        bs = inverse.shape[1]
        places = rows * SLOTS
        half = lambda *n: pltpu.VMEM(n + (bs, bs), BF16)
        hbm = pl.BlockSpec(memory_space=pl.ANY)
        vmem = pl.BlockSpec(memory_space=pltpu.VMEM)
        blocks = pl.pallas_call(
            functools.partial(sweep_kernel, rows, cols, row_devices, col_devices, bs),
            out_shape=pltpu.VMEM((places + 1, bs, bs), F32),
            in_specs=[hbm] * 5,
            out_specs=vmem,
            scratch_shapes=[
                pltpu.SMEM((rows, cols), jnp.int32), pltpu.SMEM((rows, cols), jnp.int32),
                half(places), half(cols), half(SWEEPS, 2 * rows), half(SWEEPS, 2 * rows),
                half(SWEEPS, rows), half(SWEEPS, rows),
                half(SWEEPS, rows + 1), half(SWEEPS, rows + 1), half(SWEEPS, rows), half(SWEEPS, rows),
                pltpu.VMEM((rows, bs, bs), F32),
                pltpu.SemaphoreType.DMA((2,)),
                pltpu.SemaphoreType.DMA((4,)),
                pltpu.SemaphoreType.DMA,
                pltpu.SemaphoreType.DMA,
                pltpu.SemaphoreType.DMA((SWEEPS * (rows + 7),)),
            ],
            compiler_params=pltpu.CompilerParams(collective_id=0, has_side_effects=True),
            name="sweeps",
        )(pattern, dropped, matrix, factors, inverse)
        return pl.pallas_call(
            functools.partial(place_kernel, rows, cols, row_devices, bs),
            out_shape=jax.ShapeDtypeStruct(factors.shape, F32),
            in_specs=[vmem],
            out_specs=hbm,
            scratch_shapes=[pltpu.SemaphoreType.DMA],
            name="place",
        )(pltpu.with_memory_space_constraint(blocks, pltpu.VMEM))

    placed = (P("row", "col"), P("row", "col"), P("col", None, None), P("row", "col"), P("row", "col"))
    return jax.shard_map(
        on_device, mesh=mesh, in_specs=placed, out_specs=P("row", "col"), check_vma=False
    )
```

time: 18.6 us -> 14.2 us (0.76)
  the two profiles are of different devices: /device:TPU:20 before, /device:TPU:10 now
where the time goes in v2:
time: 14.2 us; the launch traced here: 14.1 us
  Pallas kernels  14.1 us (99%)
    pallas_call x1, Pallas kernels, on_device(): pl.pallas_call(functools.partial(sweep_kernel, rows, cols, row_devices, c...  12.8 us
    pallas_call x1, Pallas kernels, on_device(): pl.pallas_call(functools.partial(place_kernel, rows, cols, row_devices, b...  1.31 us

profile of v2, /device:TPU:10, one launch (start us, length us, event | category | flops | bytes accessed | tf_op | source)
XLA Modules:
  0.0 14.1 jit_solution(1349256636763333799)
XLA Ops:
  0.0 12.8 %sweeps.1.blocks = f32[17,128,128]{2,1,0:T(8,128)S(1)} custom-call(s32[4,8]{1,0:T(4,128)} %pattern_in.1, s32[4,8]{1,0:T(4,128)} %dropped_in.1, bf16[512,1024]{1,0:T(8,128)(2,1)} %matrix.1, f32[512,1024]{1,0:T(8,128)} %factors.1, bf16[8,128,128]{2,1,0:T(8,128)(2,1)} %inverse_in.1), custom_call_target="tpu_custom_call" | custom-call | tf_op jit(solution)/shard_map/sweeps/pallas_call | solution.py:442
  12.8 1.3 %place.1 = f32[512,1024]{1,0:T(8,128)} custom-call(f32[17,128,128]{2,1,0:T(8,128)S(1)} %sweeps.1.blocks), custom_call_target="tpu_custom_call" | custom-call | tf_op jit(solution)/shard_map/place/pallas_call | solution.py:462

commit v3 on v2

--- a/solution.py
+++ b/solution.py
@@ -15,6 +15,7 @@
 SLOTS = 4
 DIAG, LEFT, RIGHT, OUTER = range(SLOTS)
 D, L_NEAR, U_NEAR, L_FAR, U_FAR = range(5)
+DETOURED = ((), ())
 
 def dot(x, y):
     return jnp.dot(x, y, preferred_element_type=F32)
@@ -106,6 +107,7 @@
         pltpu.make_async_copy(dest, dest, load_sem.at[group]).wait()
 
     odd = lax.rem(c, 2) == 1
+    aside = odd.astype(jnp.int32)
 
     def lower_step(k, b, v, diag, j, mask=None):
         product = dot(lb[v, b], diag)
@@ -166,11 +168,16 @@
         for i in range(rows):
             sd[0, i] = out[i * SLOTS + DIAG].astype(BF16)
         if near_out or far_out:
-            pl.semaphore_wait(barrier, near_out + far_out)
+            pl.semaphore_wait(barrier, near_out + far_out + bool(detour) + (aside if h and far_out and not detour else 0))
 
         def send_near(v, i):
             if near_out:
-                send(D, v, i, sd, r + 1 - detour, c + detour)
+                if detour and (v or i >= 2):
+                    send(D, v, i, sd, r, c + 1)
+                elif h and far_out and near_in and not detour and i in DETOURED[v]:
+                    send(D, v, i, sd, r + 1 - aside, c - aside)
+                else:
+                    send(D, v, i, sd, r + 1, c)
 
         def send_far(v):
             if far_out:
@@ -251,7 +258,10 @@
         drain()
 
     def lower_owner(blocks, kind, source, target):
-        hello(source[0], source[1] + (c == 0).astype(jnp.int32) if kind == L_NEAR else source[1])
+        hello(*source)
+        if kind == L_NEAR:
+            pl.when(c == 0)(lambda: hello(r - 1, c + 1))
+            pl.when(odd & (c < far_c))(lambda: hello(r - 1, c - 1))
         start_flags()
         places = [(i, s, j) for i, s, j, b, n in blocks]
         start_loads(FIRST, places)
@@ -345,8 +355,8 @@
         wait_loads(MATRIX, places)
         for i, s, j, b in blocks:
             upper_steps(i * SLOTS + s, b, masks[i * SLOTS + s])
-        send(kind, 1, 0, ub, *target)
-        send(kind, 1, 1, ub, *(second or target))
+        send(kind, 1, 0, ub, *(second or target))
+        send(kind, 1, 1, ub, *target)
         flag_copies[1].wait()
         keep(places)
         if passes is not None:
@@ -363,14 +373,31 @@
         drain()
 
     def pass_diagonal():
-        for v in range(SWEEPS):
-            pass_on(D, v, range(rows), (r + 1, c - 1))
+        pass_on(D, 0, range(2, rows), (r + 1, c - 1))
+        pass_on(D, 1, range(rows), (r + 1, c - 1))
 
     def near_passer():
-        hello(r, c + 2)
-        pl.semaphore_wait(barrier, 1)
-        pass_on(U_NEAR, 1, (1,), (r + 1, c + 2))
-        drain()
+        upper = (c + 2 >= far_c) & (c + 2 <= last)
+        diag = ~odd & (c + 1 < far_c)
+        pl.when(upper)(lambda: hello(r, c + 2))
+        pl.when(diag)(lambda: hello(r, c + 1))
+        pl.semaphore_wait(barrier, upper.astype(jnp.int32) + diag.astype(jnp.int32))
+        sent = {}
+
+        def step(when, name, *what):
+            pl.when(when)(lambda: pass_on(*what))
+            sent.setdefault(name, (when, []))[1].extend(pending)
+            pending.clear()
+
+        if DETOURED[0]:
+            step(diag, D, D, 0, DETOURED[0], (r + 1, c + 1))
+        step(upper, U_NEAR, U_NEAR, 1, (0,), (r + 1, c + 2))
+        if DETOURED[1]:
+            step(diag, D, D, 1, DETOURED[1], (r + 1, c + 1))
+        for when, own in sent.values():
+            pending.extend(own)
+            pl.when(when)(drain)
+            pending.clear()
 
     for h in (0, 1):
         pl.when((q == h) & (c == 0))(lambda: diagonal_owner(h, bool(h), False, True, True, bool(h)))
@@ -389,7 +416,7 @@
     pl.when((q == -1) & (c >= far_c))(
         lambda: upper_owner(near_upper, U_NEAR, (r + 1, c), second=(r, c - 2), passes=pass_lower)
     )
-    pl.when((q == 3) & (c + 2 >= far_c) & (c + 2 <= last))(near_passer)
+    pl.when((q == 3) & (c + 2 <= last))(near_passer)
     for h in (0, 1):
         far_lower = [(i, OUTER, h * rows + i, i, i) for i in range(rows)]
         far_upper = [(i, OUTER, h * rows + i, i) for i in range(rows)]

time: 14.2 us -> 14.1 us (level)
  the two profiles are of different devices: /device:TPU:10 before, /device:TPU:31 now
where the time goes in v3:
time: 14.1 us; the launch traced here: 13.9 us
  Pallas kernels  13.9 us (99%)
    pallas_call x1, Pallas kernels, on_device(): pl.pallas_call(functools.partial(sweep_kernel, rows, cols, row_devices, c...  12.6 us
    pallas_call x1, Pallas kernels, on_device(): pl.pallas_call(functools.partial(place_kernel, rows, cols, row_devices, b...  1.31 us

profile of v3, /device:TPU:31, one launch (start us, length us, event | category | flops | bytes accessed | tf_op | source)
XLA Modules:
  0.0 13.9 jit_solution(4259054137966813438)
XLA Ops:
  0.0 12.6 %sweeps.1.blocks = f32[17,128,128]{2,1,0:T(8,128)S(1)} custom-call(s32[4,8]{1,0:T(4,128)} %pattern_in.1, s32[4,8]{1,0:T(4,128)} %dropped_in.1, bf16[512,1024]{1,0:T(8,128)(2,1)} %matrix.1, f32[512,1024]{1,0:T(8,128)} %factors.1, bf16[8,128,128]{2,1,0:T(8,128)(2,1)} %inverse_in.1), custom_call_target="tpu_custom_call" | custom-call | tf_op jit(solution)/shard_map/sweeps/pallas_call | solution.py:469
  12.6 1.3 %place.1 = f32[512,1024]{1,0:T(8,128)} custom-call(f32[17,128,128]{2,1,0:T(8,128)S(1)} %sweeps.1.blocks), custom_call_target="tpu_custom_call" | custom-call | tf_op jit(solution)/shard_map/place/pallas_call | solution.py:489

commit v4 on v3

--- a/solution.py
+++ b/solution.py
@@ -54,17 +54,17 @@
 
     pending, seen = [], set()
 
-    def remote(kind, v, p, buf, r2, c2):
-        at = (v, pl.ds(*parts[kind][p]))
+    def remote(kind, v, p, buf, r2, c2, block=None):
+        at = (v, pl.ds(*(parts[kind][p] if block is None else (block, 1))))
         return pltpu.make_async_remote_copy(
             src_ref=buf.at[at], dst_ref=inbox[kind].at[at],
             send_sem=send_sem, recv_sem=arrival(kind, v, p),
             device_id=(r2, c2), device_id_type=MESH,
         )
 
-    def send(kind, v, p, buf, r2, c2):
-        remote(kind, v, p, buf, r2, c2).start()
-        pending.append((kind, v, p, buf))
+    def send(kind, v, p, buf, r2, c2, block=None):
+        remote(kind, v, p, buf, r2, c2, block).start()
+        pending.append((kind, v, p, buf, block))
 
     def await_part(kind, v, p):
         if (kind, v, p) not in seen:
@@ -76,8 +76,8 @@
         return inbox[kind][v, n]
 
     def drain():
-        for sent in pending:
-            remote(*sent, r ^ 1, c).wait_send()
+        for kind, v, p, buf, block in pending:
+            remote(kind, v, p, buf, r ^ 1, c, block).wait_send()
         pending.clear()
         seen.clear()
 
@@ -286,16 +286,14 @@
         wait_loads(MATRIX, places)
         inverse_copy.wait()
         for v in range(SWEEPS):
-            ds, done = {}, set()
+            ds = {}
             for i, s, j, b, n in blocks:
                 k = i * SLOTS + s
                 if n not in ds:
                     ds[n] = got(D, v, n)
                 lower_step(k, b, v, ds[n], j, masks[k])
-                done.add(b)
-                start, size = parts[kind][part_of(kind, b)]
-                if v + 1 < SWEEPS and done >= set(range(start, start + size)):
-                    send(kind, v + 1, part_of(kind, b), lb, target[0] + detour, target[1] + detour)
+                if v + 1 < SWEEPS:
+                    send(kind, v + 1, part_of(kind, b), lb, target[0] + detour, target[1] + detour, b)
         if kind != L_FAR:
             flag_copies[0].wait()
         flag_copies[1].wait()

time: 14.1 us -> 13.8 us (0.979)
  the two profiles are of different devices: /device:TPU:31 before, /device:TPU:27 now
where the time goes in v4:
time: 13.8 us; the launch traced here: 13.6 us
  Pallas kernels  13.6 us (99%)
    pallas_call x1, Pallas kernels, on_device(): pl.pallas_call(functools.partial(sweep_kernel, rows, cols, row_devices, c...  12.3 us
    pallas_call x1, Pallas kernels, on_device(): pl.pallas_call(functools.partial(place_kernel, rows, cols, row_devices, b...  1.31 us

profile of v4, /device:TPU:27, one launch (start us, length us, event | category | flops | bytes accessed | tf_op | source)
XLA Modules:
  0.0 13.6 jit_solution(15130801805525922974)
XLA Ops:
  0.0 12.3 %sweeps.1.blocks = f32[17,128,128]{2,1,0:T(8,128)S(1)} custom-call(s32[4,8]{1,0:T(4,128)} %pattern_in.1, s32[4,8]{1,0:T(4,128)} %dropped_in.1, bf16[512,1024]{1,0:T(8,128)(2,1)} %matrix.1, f32[512,1024]{1,0:T(8,128)} %factors.1, bf16[8,128,128]{2,1,0:T(8,128)(2,1)} %inverse_in.1), custom_call_target="tpu_custom_call" | custom-call | tf_op jit(solution)/shard_map/sweeps/pallas_call | solution.py:467
  12.3 1.3 %place.1 = f32[512,1024]{1,0:T(8,128)} custom-call(f32[17,128,128]{2,1,0:T(8,128)S(1)} %sweeps.1.blocks), custom_call_target="tpu_custom_call" | custom-call | tf_op jit(solution)/shard_map/place/pallas_call | solution.py:487
